TPU v7x, 32 devices: a whole 2x2x4 slice. The times are simulated.
32 devices in a mesh: gx: 8 (over y, x, core), gy: 4 (over z).
Axes of the slice: x: 2, y: 2, z: 4, core: 2. Of those that a mesh axis runs over, the one named last changes fastest.
Arguments:
- probes: bfloat16 [256, 1024, 256], P('gx', 'gy'), may hold values from -6 to 6
- blk_rows: int32 [1024, 128], P(('gx', 'gy')), may hold values from 0 to 8191
- blk_sensor: int32 [1024], P(('gx', 'gy')), may hold values from 0 to 255, as said below
- blk_count: int32 [32], P(('gx', 'gy')), may hold values from 16 to 32, as said below
- coef: bfloat16 [1024, 128], P(('gx', 'gy')), may hold values from -5 to 5
- owner: int32 [256], replicated, may hold values from 0 to 31, as said below
- weights: float32 [256], replicated, may hold values from 0.1 to 1
Outputs:
- sensitivity: float32 [256], P(('gx', 'gy'))
- new_weights: float32 [256], replicated
- density: float32 [256, 1024], P('gx', 'gy')
Inputs may be any that keep to these rules, and one draw needn't show every extreme that they name: `owner`: every device owns exactly 8 sensors. `blk_sensor`: among the live slots of one tile, at most 2 belong to sensors of one owner; in every draw some owner receives 2 live blocks from every tile. `blk_count`: some tile has all 32 slots live.
All inputs are finite; a program needn't handle non-finite values.
Results may differ from a plain program's by a relative error of at most 0.0008.
Values may be sent and summed in bfloat16 or wider, within the bound.
A program may use at most 128 MiB of HBM per device.

v0:
```python
import jax
import jax.numpy as jnp
from jax import lax
from jax.sharding import PartitionSpec as P

SPD = 8
CAP = 2


def local(probes, blk_rows, blk_sensor, blk_count, coef, owner, weights):
    size_gx = lax.axis_size("gx")
    size_gy = lax.axis_size("gy")
    n_dev = size_gx * size_gy
    me_flat = lax.axis_index("gx") * size_gy + lax.axis_index("gy")
    tile_r, tile_c, probe_n = probes.shape
    nblk, foot = blk_rows.shape
    n_sens = owner.shape[0]
    flat = probes.reshape(tile_r * tile_c, probe_n)
    picked = flat[blk_rows.reshape(-1)].reshape(nblk, foot, probe_n)
    slots = jnp.arange(nblk, dtype=jnp.int32)
    alive = slots < blk_count[0]
    dest = owner[blk_sensor]
    earlier = (dest[:, None] == dest[None, :]) & alive[None, :] & (slots[None, :] < slots[:, None])
    rank = jnp.sum(earlier.astype(jnp.int32), axis=1)
    position = jnp.where(alive, dest * CAP + rank, n_dev * CAP)
    send_rows = (
        jnp.zeros((n_dev * CAP, foot, probe_n), jnp.bfloat16).at[position].set(picked, mode="drop")
    )
    send_coef = jnp.zeros((n_dev * CAP, foot), jnp.bfloat16).at[position].set(coef, mode="drop")
    send_ids = jnp.full((n_dev * CAP,), -1, jnp.int32).at[position].set(blk_sensor, mode="drop")
    recv_rows, recv_coef, recv_ids = (
        lax.all_to_all(send_rows, ("gx", "gy"), split_axis=0, concat_axis=0, tiled=True),
        lax.all_to_all(send_coef, ("gx", "gy"), split_axis=0, concat_axis=0, tiled=True),
        lax.all_to_all(send_ids, ("gx", "gy"), split_axis=0, concat_axis=0, tiled=True),
    )
    my_ids = jnp.nonzero(owner == me_flat, size=SPD, fill_value=0)[0].astype(jnp.int32)
    select = (recv_ids[None, :] == my_ids[:, None]).astype(jnp.bfloat16)
    mixer = select[:, :, None] * recv_coef[None, :, :]
    obs = jnp.einsum("ksr,srp->krp", mixer, recv_rows, preferred_element_type=jnp.float32)
    owned = jnp.sum(obs * obs, axis=(1, 2)) / (foot * probe_n)
    spread = jnp.zeros((n_sens,), jnp.float32).at[my_ids].set(owned)
    sens_all = lax.psum(spread, ("gx", "gy"))
    gain = weights * jnp.sqrt(1.0 + sens_all)
    new_weights = n_sens * gain / jnp.sum(gain)
    values_pts = jnp.where(
        alive[:, None], new_weights[blk_sensor][:, None] * jnp.square(coef.astype(jnp.float32)), 0.0
    )
    density = (
        jnp.zeros((tile_r * tile_c,), jnp.float32)
        .at[blk_rows.reshape(-1)]
        .add(values_pts.reshape(-1))
    )
    return (owned, new_weights, density.reshape(tile_r, tile_c))


def solution(mesh):
    in_specs = (
        P("gx", "gy", None),
        P(("gx", "gy"), None),
        P(("gx", "gy")),
        P(("gx", "gy")),
        P(("gx", "gy"), None),
        P(),
        P(),
    )
    out_specs = (P(("gx", "gy")), P(), P("gx", "gy"))
    return jax.shard_map(local, mesh=mesh, in_specs=in_specs, out_specs=out_specs, check_vma=False)
```

profile of v0, /device:TPU:0, one launch (start us, length us, event | category | flops | bytes accessed | tf_op | source)
XLA Modules:
  0.0 216.0 jit_solution(14006273843416477223)
XLA Ops:
  0.6 0.7 compare_select_fusion.4
  2.0 1.4 gather_fusion
  3.4 0.2 convert_reduce_fusion
  3.5 0.8 scatter_custom_fusion.1
  4.4 0.7 all_to_all.16
  5.1 7.3 %all-to-all-start.1 = ((s32[32,2,1]{1,2,0:T(1,128)}), s32[32,2,1]{1,2,0:T(1,128)S(1)}, u32[]{:S(2)}, u32[]{:S(2)}) async-start(s32[32,2,1]{1,2,0:T(1,128)} %bitcast.7), calls=%async_computation.1 | async-start | bytes 32768 | tf_op jit(solution)/shard_map/all_to_all | solution.py:34
  12.4 0.7 compare_select_fusion
  13.1 1.4 scatter_custom_fusion.3
  14.5 5.1 %all-to-all-done.1 = s32[32,2,1]{1,2,0:T(1,128)S(1)} async-done(((s32[32,2,1]{1,2,0:T(1,128)}), s32[32,2,1]{1,2,0:T(1,128)S(1)}, u32[]{:S(2)}, u32[]{:S(2)}) %all-to-all-start.1) | async-done | bytes 288 | tf_op jit(solution)/shard_map/all_to_all | solution.py:34
  19.6 2.5 %all-to-all-start.2 = ((bf16[32,2,128]{2,1,0:T(2,128)(2,1)}), bf16[32,2,128]{2,1,0:T(2,128)(2,1)S(1)}, u32[]{:S(2)}, u32[]{:S(2)}) async-start(bf16[32,2,128]{2,1,0:T(2,128)(2,1)} %bitcast.13), calls=%async_computation.2 | async-start | bytes 32768 | tf_op jit(solution)/shard_map/all_to_all | solution.py:33
  22.2 15.7 %gather_fusion.1 = bf16[4096,256]{1,0:T(8,128)(2,1)S(1)} fusion(bf16[8192,256]{1,0:T(8,128)(2,1)} %bitcast.28, s32[4096]{0:T(1024)S(1)} %broadcast_clamp_fusion), kind=kCustom, calls=%fused_computation.1 | custom fusion | bytes 4210688 | tf_op jit(solution)/shard_map/gather | solution.py:19
  37.9 2.5 %broadcast_in_dim.36 = bf16[64,128,256]{2,1,0:T(8,128)(2,1)} broadcast(bf16[]{:T(256)} %constant.26.clone.1), dimensions={} | broadcast | bytes 4194306 | tf_op jit(solution)/shard_map/broadcast_in_dim | solution.py:27
  40.4 5.4 %scatter_fusion = bf16[64,128,256]{2,1,0:T(8,128)(2,1)} fusion(bf16[64,128,256]{2,1,0:T(8,128)(2,1)} %broadcast_in_dim.36, s32[32]{0:T(128)S(1)} %fusion.23, bf16[32,128,256]{2,1,0:T(8,128)(2,1)S(1)} %bitcast.29), kind=kCustom, calls=%fused_computation.3 | custom fusion | bytes 6291584 | tf_op jit(solution)/shard_map/scatter | solution.py:27
  45.8 0.0 copy-start
  45.8 0.0 all-to-all-done.2
  45.8 6.2 %all-to-all-start = ((bf16[64,128,256]{2,1,0:T(8,128)(2,1)}), bf16[64,128,256]{2,1,0:T(8,128)(2,1)}, u32[]{:S(2)}, u32[]{:S(2)}) async-start(bf16[64,128,256]{2,1,0:T(8,128)(2,1)} %scatter_fusion), calls=%async_computation | async-start | bytes 8388608 | tf_op jit(solution)/shard_map/all_to_all | solution.py:32
  52.0 0.0 copy-start.3
  52.0 0.0 copy-start.2
  52.0 0.0 copy-done
  52.0 0.3 reduce-window.12
  52.3 0.1 slice.7
  52.4 0.1 slice_reduce_fusion
  52.6 0.1 broadcast_add_fusion
  52.6 2.3 %scatter_custom_fusion.2 = s32[8]{0:T(128)S(1)} fusion(s32[256]{0:T(256)S(1)} %bitcast.35, s32[256]{0:T(256)S(1)} %broadcast.233, s32[]{:T(128)} %constant.27.clone.1), kind=kCustom, calls=%fused_computation.56 | custom fusion | flops 256 | bytes 36 | tf_op jit(solution)/shard_map/scatter-add | solution.py:36
  55.0 0.2 select_n.113
  55.2 0.6 fusion.17
  55.8 0.7 compare_select_fusion.10
  56.4 0.7 fusion.20
  57.1 0.5 broadcast.255
  57.6 0.7 reduce.6
  58.3 0.1 eq.43
  58.4 0.1 compare_convert_fusion
  58.5 0.1 copy.16
  58.6 85.6 %all-to-all-done = bf16[64,128,256]{2,1,0:T(8,128)(2,1)} async-done(((bf16[64,128,256]{2,1,0:T(8,128)(2,1)}), bf16[64,128,256]{2,1,0:T(8,128)(2,1)}, u32[]{:S(2)}, u32[]{:S(2)}) %all-to-all-start) | async-done | bytes 4194336 | tf_op jit(solution)/shard_map/all_to_all | solution.py:32
  144.2 4.6 %fusion.5 = f32[8]{0:T(128)S(1)} fusion(bf16[64,128,256]{2,1,0:T(8,128)(2,1)} %all-to-all-done, bf16[64,128]{0,1:T(8,128)(2,1)S(1)} %copy.16, bf16[8,64]{1,0:T(8,128)(2,1)S(1)} %compare_convert_fusion), kind=kOutput, calls=%fused_computation.12 | convolution fusion | flops 34144248 | bytes 4211744 | tf_op jit(solution)/shard_map/ksr,srp->krp/dot_general | solution.py:39
  148.8 0.0 copy-start.4
  148.8 0.6 scatter_custom_fusion.4
  149.4 42.0 %psum.7 = f32[256]{0:T(256)S(1)} all-reduce(f32[256]{0:T(256)S(1)} %scatter_custom_fusion.4), channel_id=1, replica_groups=mesh['gx'=8,'gy'=4] {'gx','gy'}, use_global_device_ids=true, to_apply=%region_11.12 | all-reduce | flops 256 | bytes 2048 | tf_op jit(solution)/shard_map/psum | solution.py:42
  191.4 0.0 copy-done.3
  191.4 0.6 fusion.28
  192.0 0.7 multiply_divide_fusion
  192.7 0.0 copy-start.1
  192.7 0.7 gather_fusion.2
  193.4 0.0 copy-done.2
  193.4 0.1 select_bitcast_fusion
  193.5 21.9 %scatter_custom_fusion.5 = f32[8192]{0:T(1024)S(1)} fusion(s32[4096]{0:T(1024)S(1)} %bitcast.32, f32[4096]{0:T(1024)S(1)} %select_bitcast_fusion, f32[]{:T(128)} %constant.76.clone.1), kind=kCustom, calls=%fused_computation.18 | custom fusion | flops 4096 | bytes 32772 | tf_op jit(solution)/shard_map/scatter-add | solution.py:51
  215.4 0.6 reshape.248
  216.0 0.0 copy-done.4
  216.0 0.0 copy-done.1
  (9 shorter events, 0.1 us)
Async XLA Ops:
  5.1 14.5 %all-to-all-start.1 = ((s32[32,2,1]{1,2,0:T(1,128)}), s32[32,2,1]{1,2,0:T(1,128)S(1)}, u32[]{:S(2)}, u32[]{:S(2)}) async-start(s32[32,2,1]{1,2,0:T(1,128)} %bitcast.7), calls=%async_computation.1 | async-start | bytes 32768 | tf_op jit(solution)/shard_map/all_to_all | solution.py:34
  19.6 26.2 %all-to-all-start.2 = ((bf16[32,2,128]{2,1,0:T(2,128)(2,1)}), bf16[32,2,128]{2,1,0:T(2,128)(2,1)S(1)}, u32[]{:S(2)}, u32[]{:S(2)}) async-start(bf16[32,2,128]{2,1,0:T(2,128)(2,1)} %bitcast.13), calls=%async_computation.2 | async-start | bytes 32768 | tf_op jit(solution)/shard_map/all_to_all | solution.py:33
  45.8 6.2 %copy-start = (s32[256]{0:T(256)S(1)}, s32[256]{0:T(256)}, u32[]{:S(2)}) copy-start(s32[256]{0:T(256)} %param.12) | copy-start | bytes 3076
  45.8 98.4 %all-to-all-start = ((bf16[64,128,256]{2,1,0:T(8,128)(2,1)}), bf16[64,128,256]{2,1,0:T(8,128)(2,1)}, u32[]{:S(2)}, u32[]{:S(2)}) async-start(bf16[64,128,256]{2,1,0:T(8,128)(2,1)} %scatter_fusion), calls=%async_computation | async-start | bytes 8388608 | tf_op jit(solution)/shard_map/all_to_all | solution.py:32
  52.0 139.4 %copy-start.3 = (f32[256]{0:T(256)S(1)}, f32[256]{0:T(256)}, u32[]{:S(2)}) copy-start(f32[256]{0:T(256)} %param.13) | copy-start | bytes 3076
  52.0 141.4 %copy-start.2 = (bf16[32,128]{1,0:T(8,128)(2,1)S(1)}, bf16[32,128]{1,0:T(8,128)(2,1)}, u32[]{:S(2)}) copy-start(bf16[32,128]{1,0:T(8,128)(2,1)} %param.11) | copy-start | bytes 24580
  148.8 67.2 %copy-start.4 = (f32[8]{0:T(128)}, f32[8]{0:T(128)S(1)}, u32[]{:S(2)}) copy-start(f32[8]{0:T(128)S(1)} %broadcast_multiply_fusion) | copy-start | bytes 100
  192.7 23.4 %copy-start.1 = (f32[256]{0:T(256)}, f32[256]{0:T(256)S(1)}, u32[]{:S(2)}) copy-start(f32[256]{0:T(256)S(1)} %multiply_divide_fusion) | copy-start | bytes 3076
where the time goes:
time: 217 us; the launch traced here: 216 us
  waiting for transfers between devices  90.6 us (42%)
  blocking collectives  42 us (19%)
  local copies, waits for them, and re-layouts  30.8 us (14%)
  other arithmetic  30.5 us (14%)
  starting transfers between devices  16.1 us (7%)
  matrix products  4.62 us (2%)
    all_to_all x1, waiting for transfers between devices, local(): lax.all_to_all(send_rows, ('gx', 'gy'), split_axis=0, concat_axis=0, tile...  85.6 us
    psum x1, blocking collectives, local(): sens_all = lax.psum(spread, ('gx', 'gy'))  42 us
    scatter-add x1, other arithmetic, local(): density = jnp.zeros((tile_r * tile_c,), jnp.float32).at[blk_rows.reshape(...  21.9 us
    gather x1, local copies, waits for them, and re-layouts, local(): picked = flat[blk_rows.reshape(-1)].reshape(nblk, foot, probe_n)  15.7 us
    all_to_all x1, starting transfers between devices, local(): lax.all_to_all(send_ids, ('gx', 'gy'), split_axis=0, concat_axis=0, tiled...  7.33 us
    all_to_all x1, starting transfers between devices, local(): lax.all_to_all(send_rows, ('gx', 'gy'), split_axis=0, concat_axis=0, tile...  6.18 us
    scatter x1, local copies, waits for them, and re-layouts, local(): jnp.zeros((n_dev * CAP, foot, probe_n), jnp.bfloat16).at[position]  5.41 us
    all_to_all x1, waiting for transfers between devices, local(): lax.all_to_all(send_ids, ('gx', 'gy'), split_axis=0, concat_axis=0, tiled...  5.05 us
  transfers between devices with their start and end apart: 3, of which 2 were waited for; matrix products, arithmetic and copies ran while one was open for 15% of the time, Pallas kernels for 0%

commit v1 on v0

v1 whole, which is shorter than its diff:
```python
import functools

import jax
import jax.numpy as jnp
from jax import lax
from jax.experimental import pallas as pl
from jax.experimental.pallas import tpu as pltpu
from jax.sharding import PartitionSpec as P

MESH = pl.DeviceIdType.MESH
F32 = jnp.float32
BF16 = jnp.bfloat16
NT = (((1,), (1,)), ((), ()))
LANES = 128


def gather_kernel(n, rows_ref, coef_ref, probes_ref, out_ref, tile_ref, stage_ref):
    tile_r, tile_c, probe_n = probes_ref.shape
    chans, nblk = stage_ref.shape[:2]

    def widen(i, carry):
        at = pl.multiple_of(i * tile_c, tile_c)
        tile_ref[pl.ds(at, tile_c), :] = probes_ref[i].astype(F32)
        return carry

    lax.fori_loop(0, tile_r, widen, 0)

    def fill(d, carry):
        for c in range(chans):
            r = d * chans + c
            for j in range(nblk):
                i = rows_ref[j, r]
                stage_ref[c, pl.ds(j, 1), :] = tile_ref[pl.ds(i, 1), :] * coef_ref[j, r]
            out_ref[d, :, c * probe_n : (c + 1) * probe_n] = stage_ref[c].astype(BF16)
        return carry

    lax.fori_loop(0, n, fill, 0)


def exchange_kernel(
    n, n_gy, scale, tile_c,
    send_ref, ids_ref, ids_col_ref, rows_ref, coef_ref, owner_ref, weights_ref,
    owned_ref, new_ref, density_ref,
    recv_ref, ids_recv, obs_ref, planes_ref, h_send, h_recv,
    send_sem, recv_sem, ids_send_sem, ids_recv_sem, h_send_sem, h_recv_sem,
):
    me = lax.axis_index("gx") * n_gy + lax.axis_index("gy")
    nblk, width = send_ref.shape[1:]
    n_sens = owner_ref.shape[1]
    tile_r = density_ref.shape[0]
    share = max(1, LANES // nblk)

    def peer(k):
        t = lax.rem(me + k, n)
        return t, (t // n_gy, lax.rem(t, n_gy))

    barrier = pltpu.get_barrier_semaphore()

    def greet(k, carry):
        pl.semaphore_signal(barrier, inc=1, device_id=peer(k)[1], device_id_type=MESH)
        return carry

    lax.fori_loop(1, n, greet, 0)
    own = pltpu.make_async_copy(send_ref.at[me], recv_ref.at[me], recv_sem.at[me])
    own_ids = pltpu.make_async_copy(ids_ref, ids_recv.at[me], ids_recv_sem.at[me])
    own.start()
    own_ids.start()
    pl.semaphore_wait(barrier, n - 1)

    def block_copy(k):
        t, where = peer(k)
        return pltpu.make_async_remote_copy(
            src_ref=send_ref.at[t], dst_ref=recv_ref.at[me],
            send_sem=send_sem.at[k], recv_sem=recv_sem.at[me],
            device_id=where, device_id_type=MESH,
        )

    def ids_copy(k):
        return pltpu.make_async_remote_copy(
            src_ref=ids_ref, dst_ref=ids_recv.at[me],
            send_sem=ids_send_sem.at[k], recv_sem=ids_recv_sem.at[me],
            device_id=peer(k)[1], device_id_type=MESH,
        )

    def h_copy(k):
        return pltpu.make_async_remote_copy(
            src_ref=h_send, dst_ref=h_recv.at[me],
            send_sem=h_send_sem.at[k], recv_sem=h_recv_sem.at[me],
            device_id=peer(k)[1], device_id_type=MESH,
        )

    def launch(k, carry):
        ids_copy(k).start()
        block_copy(k).start()
        return carry

    lax.fori_loop(1, n, launch, 0)

    def plane(j, carry):
        at = rows_ref[pl.ds(j, 1), :]
        c = coef_ref[pl.ds(j, 1), :]
        square = c * c
        top = square.astype(BF16).astype(F32)
        high = at // tile_c
        low = at - high * tile_c
        here = high == lax.broadcasted_iota(jnp.int32, (tile_r, at.shape[1]), 0)
        left = jnp.concatenate(
            [jnp.where(here, top, 0.0), jnp.where(here, square - top, 0.0)], axis=0
        ).astype(BF16)
        right = jnp.where(
            low == lax.broadcasted_iota(jnp.int32, (tile_c, at.shape[1]), 0), 1.0, 0.0
        ).astype(BF16)
        both = lax.dot_general(left, right, NT, preferred_element_type=F32)
        planes_ref[j] = both[:tile_r] + both[tile_r:]
        return carry

    lax.fori_loop(0, nblk, plane, 0)

    spd = n_sens // n
    mine = jnp.where(owner_ref[...] == me, 1.0, 0.0)
    before = jnp.where(
        lax.broadcasted_iota(jnp.int32, (n_sens, n_sens), 0)
        < lax.broadcasted_iota(jnp.int32, (n_sens, n_sens), 1),
        1.0, 0.0,
    ).astype(BF16)
    rank = jnp.dot(
        jnp.broadcast_to(mine, (spd, n_sens)).astype(BF16), before, preferred_element_type=F32
    )
    place = lax.broadcasted_iota(jnp.int32, (spd, n_sens), 0).astype(F32)
    select = jnp.where(rank == place, 1.0, 0.0) * mine

    def ids_wait(t, carry):
        pltpu.make_async_copy(ids_ref, ids_recv.at[t], ids_recv_sem.at[t]).wait()
        return carry

    lax.fori_loop(0, n, ids_wait, 0)

    group = max(1, 256 // nblk)
    depth = group * nblk
    obs_ref[...] = jnp.zeros_like(obs_ref)

    def mix(g, carry):
        pieces = []
        for piece in range(depth // LANES):
            row = ids_recv[g * group + piece * share]
            for extra in range(1, share):
                row = row + ids_recv[g * group + piece * share + extra]
            pieces.append(row)
        ids_row = jnp.concatenate(pieces, axis=1)
        mixer = jnp.where(
            ids_row == lax.broadcasted_iota(jnp.int32, (n_sens, depth), 0) + 1, 1.0, 0.0
        ).astype(BF16)
        for piece in range(group):
            t = g * group + piece
            pltpu.make_async_copy(send_ref.at[0], recv_ref.at[t], recv_sem.at[t]).wait()
        block = recv_ref[pl.ds(g * group, group)].reshape(depth, width)
        obs_ref[...] += jnp.dot(mixer, block, preferred_element_type=F32)
        return carry

    lax.fori_loop(0, n // group, mix, 0)

    eye = lax.broadcasted_iota(jnp.int32, (LANES, LANES), 0) == lax.broadcasted_iota(
        jnp.int32, (LANES, LANES), 1
    )
    for b in range(n_sens // LANES):
        x = obs_ref[b * LANES : (b + 1) * LANES, :]
        s = jnp.sum(x * x, axis=1, keepdims=True)
        h_send[:, b * LANES : (b + 1) * LANES] = jnp.sum(
            jnp.where(eye, s, 0.0), axis=0, keepdims=True
        )
    h_recv[me] = h_send[...]

    def h_launch(k, carry):
        h_copy(k).start()
        return carry

    lax.fori_loop(1, n, h_launch, 0)

    def h_wait(k, carry):
        t = peer(k)[0]
        pltpu.make_async_copy(h_send, h_recv.at[t], h_recv_sem.at[t]).wait()
        return carry

    lax.fori_loop(1, n, h_wait, 0)
    h = jnp.sum(h_recv[...], axis=0) * scale
    gain = weights_ref[...] * jnp.sqrt(1.0 + h)
    new = n_sens * gain / jnp.sum(gain, axis=1, keepdims=True)
    new_ref[...] = new
    owned_ref[...] = jnp.sum(select * h, axis=1, keepdims=True)
    lookup = (
        ids_col_ref[...] == lax.broadcasted_iota(jnp.int32, (nblk, n_sens), 1) + 1
    )
    factor = jnp.sum(jnp.where(lookup, new, 0.0), axis=1, keepdims=True)
    total = factor[0:1] * planes_ref[0]
    for j in range(1, nblk):
        total = total + factor[j : j + 1] * planes_ref[j]
    density_ref[...] = total

    def drain(k, carry):
        block_copy(k).wait_send()
        ids_copy(k).wait_send()
        h_copy(k).wait_send()
        return carry

    lax.fori_loop(1, n, drain, 0)


def local(n, n_gy, probes, blk_rows, blk_sensor, blk_count, coef, owner, weights):
    tile_r, tile_c, probe_n = probes.shape
    nblk, foot = blk_rows.shape
    n_sens = owner.shape[0]
    chans = foot // n
    width = chans * probe_n
    me = lax.axis_index("gx") * n_gy + lax.axis_index("gy")
    coef32 = coef.astype(F32)
    slots = jnp.arange(nblk, dtype=jnp.int32)
    ids = jnp.where(slots < blk_count[0], blk_sensor + 1, 0)
    share = max(1, LANES // nblk)
    part = jnp.arange(share, dtype=jnp.int32)[:, None] == me % share
    ids_row = jnp.where(part, ids[None, :], 0).reshape(1, share * nblk)

    vmem = pl.BlockSpec(memory_space=pltpu.VMEM)
    smem = pl.BlockSpec(memory_space=pltpu.SMEM)
    send = pl.pallas_call(
        functools.partial(gather_kernel, n),
        out_shape=jax.ShapeDtypeStruct((n, nblk, width), BF16),
        in_specs=[smem, smem, vmem],
        out_specs=vmem,
        scratch_shapes=[
            pltpu.VMEM((tile_r * tile_c, probe_n), F32),
            pltpu.VMEM((chans, nblk, probe_n), F32),
        ],
        compiler_params=pltpu.CompilerParams(vmem_limit_bytes=40 * 2**20),
        name="gather_rows",
    )(blk_rows, coef32, probes)

    dma = pltpu.SemaphoreType.DMA
    owned, new, density = pl.pallas_call(
        functools.partial(exchange_kernel, n, n_gy, 1.0 / (foot * probe_n), tile_c),
        out_shape=(
            jax.ShapeDtypeStruct((n_sens // n, 1), F32),
            jax.ShapeDtypeStruct((1, n_sens), F32),
            jax.ShapeDtypeStruct((tile_r, tile_c), F32),
        ),
        in_specs=[vmem] * 7,
        out_specs=(vmem, vmem, vmem),
        scratch_shapes=[
            pltpu.VMEM((n, nblk, width), BF16),
            pltpu.VMEM((n, 1, share * nblk), jnp.int32),
            pltpu.VMEM((n_sens, width), F32),
            pltpu.VMEM((nblk, tile_r, tile_c), F32),
            pltpu.VMEM((1, n_sens), F32),
            pltpu.VMEM((n, 1, n_sens), F32),
            dma((n,)), dma((n,)), dma((n,)), dma((n,)), dma((n,)), dma((n,)),
        ],
        compiler_params=pltpu.CompilerParams(
            collective_id=0, has_side_effects=True, vmem_limit_bytes=48 * 2**20
        ),
        name="exchange_mix",
    )(
        send, ids_row, ids.reshape(nblk, 1), blk_rows, coef32,
        owner.reshape(1, n_sens), weights.reshape(1, n_sens),
    )
    return owned.reshape(-1), new.reshape(-1), density


def solution(mesh):
    n_gy = mesh.shape["gy"]
    n = mesh.shape["gx"] * n_gy
    in_specs = (
        P("gx", "gy", None),
        P(("gx", "gy"), None),
        P(("gx", "gy")),
        P(("gx", "gy")),
        P(("gx", "gy"), None),
        P(),
        P(),
    )
    out_specs = (P(("gx", "gy")), P(), P("gx", "gy"))
    return jax.shard_map(
        functools.partial(local, n, n_gy),
        mesh=mesh, in_specs=in_specs, out_specs=out_specs, check_vma=False,
    )
```

time: 217 us -> 83.6 us (0.39)
  waiting for transfers between devices: 90.6 us -> 0 us
  Pallas kernels: 0 us -> 74.9 us
  blocking collectives: 42 us -> 0 us
  other arithmetic: 30.5 us -> 2.73 us
  local copies, waits for them, and re-layouts: 30.8 us -> 4.27 us
  starting transfers between devices: 16.1 us -> 0 us
  matrix products: 4.62 us -> 0 us
    all_to_all x3 -> x0, waiting for transfers between devices: 90.6 us -> none  [the longest x1 85.6 us: local(): lax.all_to_all(send_rows, ('gx', 'gy'), split_axis=0, concat_axis=0, tile...]
    pallas_call x0 -> x2, Pallas kernels: none -> 74.9 us  [the longest x1 62.6 us: local(): pl.pallas_call(functools.partial(exchange_kernel, n, n_gy, 1.0 / (foot *...]
    psum x1 -> x0, blocking collectives: 42 us -> none  [local(): sens_all = lax.psum(spread, ('gx', 'gy'))]
    scatter-add x2 -> x0, other arithmetic: 24.2 us -> none  [the longest x1 21.9 us: local(): density = jnp.zeros((tile_r * tile_c,), jnp.float32).at[blk_rows.reshape(...]
    gather x3 -> x0, local copies, waits for them, and re-layouts: 17.8 us -> none  [the longest x1 15.7 us: local(): picked = flat[blk_rows.reshape(-1)].reshape(nblk, foot, probe_n)]
    all_to_all x3 -> x0, starting transfers between devices: 16.1 us -> none  [the longest x1 7.33 us: local(): lax.all_to_all(send_ids, ('gx', 'gy'), split_axis=0, concat_axis=0, tiled...]
    scatter x4 -> x0, local copies, waits for them, and re-layouts: 8.22 us -> none  [the longest x1 5.41 us: local(): jnp.zeros((n_dev * CAP, foot, probe_n), jnp.bfloat16).at[position]]
    dot_general x1 -> x0, matrix products: 4.62 us -> none  [local(): jnp.einsum('ksr,srp->krp', mixer, recv_rows, preferred_element_type=jnp.f...]
  transfers between devices with their start and end apart: 3 -> 0, of which waited for: 2 -> 0; matrix products, arithmetic and copies ran while one was open for 15% -> 0% of each run, Pallas kernels for 0% -> 0%
where the time goes in v1:
time: 83.6 us; the launch traced here: 83.3 us
  Pallas kernels  74.9 us (90%)
  local copies, waits for them, and re-layouts  4.27 us (5%)
  other arithmetic  2.73 us (3%)
  between operations  1.37 us (2%)
    pallas_call x1, Pallas kernels, local(): pl.pallas_call(functools.partial(exchange_kernel, n, n_gy, 1.0 / (foot *...  62.6 us
    pallas_call x1, Pallas kernels, local(): pl.pallas_call(functools.partial(gather_kernel, n), out_shape=jax.ShapeDt...  12.3 us
    unnamed x12, local copies, waits for them, and re-layouts  4.1 us

profile of v1, /device:TPU:0, one launch (start us, length us, event | category | flops | bytes accessed | tf_op | source)
XLA Modules:
  0.0 83.3 jit_solution(368244992592301060)
XLA Ops:
  0.6 0.0 copy-start.2
  0.6 0.0 copy-start.4
  0.7 0.0 copy-start.3
  1.3 0.7 fusion
  2.0 0.7 compare_select_fusion
  2.7 0.1 broadcast_select_fusion
  2.7 0.1 select_n.28.ids_ref
  2.8 0.1 copy.11.ids_col_ref
  2.9 0.7 convert_element_type.3.coef_ref
  3.6 0.0 copy-start
  3.6 2.2 %copy-done = bf16[32,256,256]{2,1,0:T(8,128)(2,1)S(1)} copy-done((bf16[32,256,256]{2,1,0:T(8,128)(2,1)S(1)}, bf16[32,256,256]{2,1,0:T(8,128)(2,1)}, u32[]{:S(2)}) %copy-start) | copy-done | bytes 4194328
  5.8 0.0 copy-start.1
  5.8 0.7 copy-done.1
  6.5 12.3 %gather_rows.1.send_ref = bf16[32,32,1024]{2,1,0:T(8,128)(2,1)S(1)} custom-call(s32[32,128]{1,0:T(8,128)S(1)} %copy-done.1, f32[32,128]{1,0:T(8,128)S(1)} %convert_element_type.3.coef_ref, bf16[32,256,256]{2,1,0:T(8,128)(2,1)S(1)} %copy-done), custom_call_target="tpu_custom_call" | custom-call | tf_op jit(solution)/shard_map/gather_rows/pallas_call | solution.py:224
  18.8 0.0 copy-done.2
  18.9 0.0 copy-done.4
  18.9 0.0 copy-done.3
  18.9 62.6 %exchange_mix.1 = (f32[8,1]{1,0:T(8,128)S(1)}, f32[1,256]{1,0:T(1,128)S(1)}, f32[32,256]{1,0:T(8,128)S(1)}) custom-call(bf16[32,32,1024]{2,1,0:T(8,128)(2,1)S(1)} %gather_rows.1.send_ref, s32[1,128]{1,0:T(1,128)S(1)} %select_n.28.ids_ref, s32[32,1]{1,0:T(8,128)S(1)} %copy.11.ids_col_ref, s32[32,128]{1,0:T(8,128)S(1)} %copy-done.2, ...), custom_call_target="tpu_custom_call" | custom-call | tf_op jit(solution)/shard_map/exchange_mix/pallas_call | solution.py:238
  81.5 0.6 reduce
  82.1 0.6 copy.15
  82.7 0.6 copy.16
  (1 shorter events, 0.0 us)
Async XLA Ops:
  0.6 18.2 %copy-start.2 = (s32[32,128]{1,0:T(8,128)S(1)}, s32[32,128]{1,0:T(8,128)}, u32[]{:S(2)}) copy-start(s32[32,128]{1,0:T(8,128)} %rows_ref.3) | copy-start | bytes 49156
  0.6 18.2 %copy-start.4 = (f32[256]{0:T(256)S(1)}, f32[256]{0:T(256)}, u32[]{:S(2)}) copy-start(f32[256]{0:T(256)} %param.13) | copy-start | bytes 3076
  0.7 18.2 %copy-start.3 = (s32[256]{0:T(256)S(1)}, s32[256]{0:T(256)}, u32[]{:S(2)}) copy-start(s32[256]{0:T(256)} %param.12) | copy-start | bytes 3076
  3.6 2.2 %copy-start = (bf16[32,256,256]{2,1,0:T(8,128)(2,1)S(1)}, bf16[32,256,256]{2,1,0:T(8,128)(2,1)}, u32[]{:S(2)}) copy-start(bf16[32,256,256]{2,1,0:T(8,128)(2,1)} %probes_ref.1) | copy-start | bytes 12582916
  5.8 0.7 copy-start.1

commit v2 on v1

v2 whole, which is shorter than its diff:
```python
import functools

import jax
import jax.numpy as jnp
from jax import lax
from jax.experimental import pallas as pl
from jax.experimental.pallas import tpu as pltpu
from jax.sharding import PartitionSpec as P

MESH = pl.DeviceIdType.MESH
F32 = jnp.float32
BF16 = jnp.bfloat16
NT = (((1,), (1,)), ((), ()))
LANES = 128


def step_kernel(
    n, n_gy, scale,
    rows_sm, count_sm, probes_hbm, sensor_ref, rows_ref, coef_ref, owner_ref, weights_ref,
    owned_ref, new_ref, density_ref,
    probes_ref, tile_ref, stage_ref, coef32_ref, send_ref, recv_ref, ids_send, ids_recv,
    obs_ref, planes_ref, h_send, h_recv,
    load_sem, send_sem, recv_sem, ids_send_sem, ids_recv_sem, h_send_sem, h_recv_sem,
):
    me = lax.axis_index("gx") * n_gy + lax.axis_index("gy")
    nblk, width = send_ref.shape[1:]
    tile_r, tile_c, probe_n = probes_ref.shape
    chans = stage_ref.shape[0]
    n_sens = owner_ref.shape[1]
    foot = coef_ref.shape[1]
    wide = ids_send.shape[1]
    share = wide // nblk

    def peer(k):
        t = lax.rem(me + k, n)
        return t, (t // n_gy, lax.rem(t, n_gy))

    barrier = pltpu.get_barrier_semaphore()

    def greet(k, carry):
        pl.semaphore_signal(barrier, inc=1, device_id=peer(k)[1], device_id_type=MESH)
        return carry

    parts = load_sem.shape[0]
    span = tile_r // parts

    def load(q):
        at = pl.ds(q * span, span)
        return pltpu.make_async_copy(probes_hbm.at[at], probes_ref.at[at], load_sem.at[q])

    for q in range(parts):
        load(q).start()
    lax.fori_loop(1, n, greet, 0)

    coef32_ref[...] = coef_ref[...].astype(F32)
    slot = lax.broadcasted_iota(jnp.int32, (1, nblk), 1)
    ids_one = jnp.where(slot < count_sm[0], sensor_ref[...] + 1, 0).astype(F32)
    down = lax.broadcasted_iota(jnp.int32, (nblk, nblk), 0)
    ids_col = jnp.sum(
        jnp.where(down == lax.broadcasted_iota(jnp.int32, (nblk, nblk), 1), ids_one, 0.0),
        axis=1, keepdims=True,
    )
    offset = lax.rem(me, share) * nblk
    ids_send[...] = jnp.sum(
        jnp.where(
            lax.broadcasted_iota(jnp.int32, (nblk, wide), 1)
            == lax.broadcasted_iota(jnp.int32, (nblk, wide), 0) + offset,
            ids_col, 0.0,
        ),
        axis=0, keepdims=True,
    )
    ids_recv[me] = ids_send[...]

    for q in range(parts):
        load(q).wait()

        def widen(i, carry):
            at = pl.multiple_of(i * tile_c, tile_c)
            tile_ref[pl.ds(at, tile_c), :] = probes_ref[i].astype(F32)
            return carry

        lax.fori_loop(q * span, (q + 1) * span, widen, 0)

    pl.semaphore_wait(barrier, n - 1)

    def block_copy(k):
        t, where = peer(k)
        return pltpu.make_async_remote_copy(
            src_ref=send_ref.at[t], dst_ref=recv_ref.at[me],
            send_sem=send_sem.at[k], recv_sem=recv_sem.at[me],
            device_id=where, device_id_type=MESH,
        )

    def ids_copy(k):
        return pltpu.make_async_remote_copy(
            src_ref=ids_send, dst_ref=ids_recv.at[me],
            send_sem=ids_send_sem.at[k], recv_sem=ids_recv_sem.at[me],
            device_id=peer(k)[1], device_id_type=MESH,
        )

    def h_copy(k):
        return pltpu.make_async_remote_copy(
            src_ref=h_send, dst_ref=h_recv.at[me],
            send_sem=h_send_sem.at[k], recv_sem=h_recv_sem.at[me],
            device_id=peer(k)[1], device_id_type=MESH,
        )

    channel = lax.broadcasted_iota(jnp.int32, (nblk, foot), 1)

    def gather(d):
        for c in range(chans):
            r = d * chans + c
            for j in range(nblk):
                i = rows_sm[j, r]
                stage_ref[c, pl.ds(j, 1), :] = tile_ref[pl.ds(i, 1), :]
            column = jnp.sum(
                jnp.where(channel == r, coef32_ref[...], 0.0), axis=1, keepdims=True
            )
            send_ref[d, :, c * probe_n : (c + 1) * probe_n] = (stage_ref[c] * column).astype(BF16)

    def launch(k, carry):
        gather(peer(k)[0])

        @pl.when(k > 1)
        def _():
            block_copy(k - 1).start()
            ids_copy(k - 1).start()

        return carry

    lax.fori_loop(1, n + 1, launch, 0)
    own = pltpu.make_async_copy(send_ref.at[me], recv_ref.at[me], recv_sem.at[me])

    def plane(j, carry):
        at = rows_ref[pl.ds(j, 1), :]
        c = coef32_ref[pl.ds(j, 1), :]
        square = c * c
        top = square.astype(BF16).astype(F32)
        high = at // tile_c
        low = at - high * tile_c
        here = high == lax.broadcasted_iota(jnp.int32, (tile_r, foot), 0)
        left = jnp.concatenate(
            [jnp.where(here, top, 0.0), jnp.where(here, square - top, 0.0)], axis=0
        ).astype(BF16)
        right = jnp.where(
            low == lax.broadcasted_iota(jnp.int32, (tile_c, foot), 0), 1.0, 0.0
        ).astype(BF16)
        both = lax.dot_general(left, right, NT, preferred_element_type=F32)
        planes_ref[j] = both[:tile_r] + both[tile_r:]
        return carry

    lax.fori_loop(0, nblk, plane, 0)
    own.start()

    spd = n_sens // n
    mine = jnp.where(owner_ref[...] == me, 1.0, 0.0)
    before = jnp.where(
        lax.broadcasted_iota(jnp.int32, (n_sens, n_sens), 0)
        < lax.broadcasted_iota(jnp.int32, (n_sens, n_sens), 1),
        1.0, 0.0,
    ).astype(BF16)
    rank = jnp.dot(
        jnp.broadcast_to(mine, (spd, n_sens)).astype(BF16), before, preferred_element_type=F32
    )
    place = lax.broadcasted_iota(jnp.int32, (spd, n_sens), 0).astype(F32)
    select = jnp.where(rank == place, 1.0, 0.0) * mine

    def ids_wait(k, carry):
        t = peer(k)[0]
        pltpu.make_async_copy(ids_send, ids_recv.at[t], ids_recv_sem.at[t]).wait()
        return carry

    lax.fori_loop(1, n, ids_wait, 0)

    group = max(1, 256 // nblk)
    depth = group * nblk
    obs_ref[...] = jnp.zeros_like(obs_ref)
    sensor_up = (lax.broadcasted_iota(jnp.int32, (n_sens, depth), 0) + 1).astype(F32)

    def mix(g, carry):
        pieces = []
        for piece in range(depth // wide):
            row = ids_recv[g * group + piece * share]
            for extra in range(1, share):
                row = row + ids_recv[g * group + piece * share + extra]
            pieces.append(row)
        ids_row = jnp.concatenate(pieces, axis=1)
        mixer = jnp.where(ids_row == sensor_up, 1.0, 0.0).astype(BF16)
        for piece in range(group):
            t = g * group + piece
            pltpu.make_async_copy(send_ref.at[0], recv_ref.at[t], recv_sem.at[t]).wait()
        block = recv_ref[pl.ds(g * group, group)].reshape(depth, width)
        obs_ref[...] += jnp.dot(mixer, block, preferred_element_type=F32)
        return carry

    lax.fori_loop(0, n // group, mix, 0)

    eye = lax.broadcasted_iota(jnp.int32, (LANES, LANES), 0) == lax.broadcasted_iota(
        jnp.int32, (LANES, LANES), 1
    )
    for b in range(n_sens // LANES):
        x = obs_ref[b * LANES : (b + 1) * LANES, :]
        s = jnp.sum(x * x, axis=1, keepdims=True)
        h_send[:, b * LANES : (b + 1) * LANES] = jnp.sum(
            jnp.where(eye, s, 0.0), axis=0, keepdims=True
        )
    h_recv[me] = h_send[...]

    def h_launch(k, carry):
        h_copy(k).start()
        return carry

    lax.fori_loop(1, n, h_launch, 0)

    def drain(k, carry):
        block_copy(k).wait_send()
        ids_copy(k).wait_send()
        return carry

    lax.fori_loop(1, n, drain, 0)

    def h_wait(k, carry):
        t = peer(k)[0]
        pltpu.make_async_copy(h_send, h_recv.at[t], h_recv_sem.at[t]).wait()
        return carry

    lax.fori_loop(1, n, h_wait, 0)
    h = jnp.sum(h_recv[...], axis=0) * scale
    gain = weights_ref[...] * jnp.sqrt(1.0 + h)
    new = n_sens * gain / jnp.sum(gain, axis=1, keepdims=True)
    new_ref[...] = new
    owned = jnp.sum(select * h, axis=1, keepdims=True)
    small = lax.broadcasted_iota(jnp.int32, (spd, spd), 0) == lax.broadcasted_iota(
        jnp.int32, (spd, spd), 1
    )
    owned_ref[...] = jnp.sum(jnp.where(small, owned, 0.0), axis=0, keepdims=True)
    lookup = ids_col == (lax.broadcasted_iota(jnp.int32, (nblk, n_sens), 1) + 1).astype(F32)
    factor = jnp.sum(jnp.where(lookup, new, 0.0), axis=1, keepdims=True)
    total = factor[0:1] * planes_ref[0]
    for j in range(1, nblk):
        total = total + factor[j : j + 1] * planes_ref[j]
    density_ref[...] = total

    def h_drain(k, carry):
        h_copy(k).wait_send()
        return carry

    lax.fori_loop(1, n, h_drain, 0)


def local(n, n_gy, probes, blk_rows, blk_sensor, blk_count, coef, owner, weights):
    tile_r, tile_c, probe_n = probes.shape
    nblk, foot = blk_rows.shape
    n_sens = owner.shape[0]
    chans = foot // n
    width = chans * probe_n
    wide = max(LANES, nblk)

    vmem = pl.BlockSpec(memory_space=pltpu.VMEM)
    smem = pl.BlockSpec(memory_space=pltpu.SMEM)
    dma = pltpu.SemaphoreType.DMA
    owned, new, density = pl.pallas_call(
        functools.partial(step_kernel, n, n_gy, 1.0 / (foot * probe_n)),
        out_shape=(
            jax.ShapeDtypeStruct((1, n_sens // n), F32),
            jax.ShapeDtypeStruct((1, n_sens), F32),
            jax.ShapeDtypeStruct((tile_r, tile_c), F32),
        ),
        in_specs=[smem, smem, pl.BlockSpec(memory_space=pl.ANY)] + [vmem] * 5,
        out_specs=(vmem, vmem, vmem),
        scratch_shapes=[
            pltpu.VMEM((tile_r, tile_c, probe_n), BF16),
            pltpu.VMEM((tile_r * tile_c, probe_n), F32),
            pltpu.VMEM((chans, nblk, probe_n), F32),
            pltpu.VMEM((nblk, foot), F32),
            pltpu.VMEM((n, nblk, width), BF16),
            pltpu.VMEM((n, nblk, width), BF16),
            pltpu.VMEM((1, wide), F32),
            pltpu.VMEM((n, 1, wide), F32),
            pltpu.VMEM((n_sens, width), F32),
            pltpu.VMEM((nblk, tile_r, tile_c), F32),
            pltpu.VMEM((1, n_sens), F32),
            pltpu.VMEM((n, 1, n_sens), F32),
            dma((4,)), dma((n,)), dma((n,)), dma((n,)), dma((n,)), dma((n,)), dma((n,)),
        ],
        compiler_params=pltpu.CompilerParams(
            collective_id=0, has_side_effects=True, vmem_limit_bytes=61 * 2**20
        ),
        name="reweight_step",
    )(
        blk_rows, blk_count, probes, blk_sensor.reshape(1, nblk), blk_rows, coef,
        owner.reshape(1, n_sens), weights.reshape(1, n_sens),
    )
    return owned.reshape(-1), new.reshape(-1), density


def solution(mesh):
    n_gy = mesh.shape["gy"]
    n = mesh.shape["gx"] * n_gy
    in_specs = (
        P("gx", "gy", None),
        P(("gx", "gy"), None),
        P(("gx", "gy")),
        P(("gx", "gy")),
        P(("gx", "gy"), None),
        P(),
        P(),
    )
    out_specs = (P(("gx", "gy")), P(), P("gx", "gy"))
    return jax.shard_map(
        functools.partial(local, n, n_gy),
        mesh=mesh, in_specs=in_specs, out_specs=out_specs, check_vma=False,
    )
```

time: 83.6 us -> 70.7 us (0.85)
  Pallas kernels: 74.9 us -> 65.3 us
  other arithmetic: 2.73 us -> 0 us
    pallas_call x2 -> x1, Pallas kernels: 74.9 us -> 65.3 us  [local(): pl.pallas_call(functools.partial(step_kernel, n, n_gy, 1.0 / (foot * prob...]
    unnamed x12 -> x3, local copies, waits for them, and re-layouts: 4.1 us -> 3.75 us
where the time goes in v2:
time: 70.7 us; the launch traced here: 70.4 us
  Pallas kernels  65.3 us (92%)
  local copies, waits for them, and re-layouts  3.75 us (5%)
  between operations  1.29 us (2%)
    pallas_call x1, Pallas kernels, local(): pl.pallas_call(functools.partial(step_kernel, n, n_gy, 1.0 / (foot * prob...  65.3 us
    unnamed x3, local copies, waits for them, and re-layouts  3.75 us

profile of v2, /device:TPU:0, one launch (start us, length us, event | category | flops | bytes accessed | tf_op | source)
XLA Modules:
  0.0 70.4 jit_solution(18338282835685621013)
XLA Ops:
  1.3 65.3 %reweight_step.1 = (f32[1,8]{1,0:T(1,128)}, f32[1,256]{1,0:T(1,128)}, f32[32,256]{1,0:T(8,128)}) custom-call(s32[32,128]{1,0:T(8,128)} %rows_ref.1, s32[1]{0:T(128)S(6)} %copy.13.count_sm, bf16[32,256,256]{2,1,0:T(8,128)(2,1)} %probes_hbm.1, s32[1,32]{1,0:T(1,128)} %bitcast.8, s32[32,128]{1,0:T(8,128)} %rows_ref.1, bf16[32,128]{1,0:T(8,128)(2,1)} %coef_ref.1, ...), custom_call_target="tpu_custom_call" | custom-call | tf_op jit(solution)/shard_map/reweight_step/pallas_call | solution.py:262
  66.6 1.1 %copy.14 = f32[8]{0:T(128)} copy(f32[8]{0:T(128)} %bitcast.9) | data formatting | bytes 64
  67.8 1.2 %copy.15 = f32[256]{0:T(256)} copy(f32[256]{0:T(256)} %bitcast.7) | data formatting | bytes 2048
  69.0 1.4 %copy.16 = f32[32,256]{1,0:T(8,128)} copy(f32[32,256]{1,0:T(8,128)} %get-tuple-element.14) | data formatting | bytes 65536

commit v3 on v2

--- a/solution.py
+++ b/solution.py
@@ -21,19 +21,36 @@
     probes_ref, tile_ref, stage_ref, coef32_ref, send_ref, recv_ref, ids_send, ids_recv,
     obs_ref, planes_ref, h_send, h_recv,
     load_sem, send_sem, recv_sem, ids_send_sem, ids_recv_sem, h_send_sem, h_recv_sem,
+    *merge_refs,
 ):
-    me = lax.axis_index("gx") * n_gy + lax.axis_index("gy")
+    m, hz = n // 2, n_gy // 2
+    half = lax.axis_index("gy") // hz
+    inner = lax.axis_index("gx") * hz + lax.rem(lax.axis_index("gy"), hz)
+    me = half * m + inner
+    flat = lax.axis_index("gx") * n_gy + lax.axis_index("gy")
     nblk, width = send_ref.shape[1:]
     tile_r, tile_c, probe_n = probes_ref.shape
-    chans = stage_ref.shape[0]
+    chans = width // probe_n
+    merge = bool(merge_refs)
+    if merge:
+        (send_m, recv_m, obs_m, part_send, part_recv,
+         send_m_sem, recv_m_sem, part_send_sem, part_recv_sem) = merge_refs
+        chans_m = send_m.shape[2] // probe_n
+        side = part_send.shape[1]
+    else:
+        chans_m = 0
     n_sens = owner_ref.shape[1]
     foot = coef_ref.shape[1]
     wide = ids_send.shape[1]
     share = wide // nblk
 
+    def device_of(t):
+        q = lax.rem(t, m)
+        return (q // hz, (t // m) * hz + lax.rem(q, hz))
+
     def peer(k):
         t = lax.rem(me + k, n)
-        return t, (t // n_gy, lax.rem(t, n_gy))
+        return t, device_of(t)
 
     barrier = pltpu.get_barrier_semaphore()
 
@@ -83,12 +100,25 @@
 
     pl.semaphore_wait(barrier, n - 1)
 
-    def block_copy(k):
-        t, where = peer(k)
+    def block_copy(t):
         return pltpu.make_async_remote_copy(
             src_ref=send_ref.at[t], dst_ref=recv_ref.at[me],
-            send_sem=send_sem.at[k], recv_sem=recv_sem.at[me],
-            device_id=where, device_id_type=MESH,
+            send_sem=send_sem.at[t], recv_sem=recv_sem.at[me],
+            device_id=device_of(t), device_id_type=MESH,
+        )
+
+    def merge_copy(q):
+        return pltpu.make_async_remote_copy(
+            src_ref=send_m.at[q], dst_ref=recv_m.at[inner],
+            send_sem=send_m_sem.at[q], recv_sem=recv_m_sem.at[inner],
+            device_id=device_of(half * m + q), device_id_type=MESH,
+        )
+
+    def part_copy():
+        return pltpu.make_async_remote_copy(
+            src_ref=part_send, dst_ref=part_recv,
+            send_sem=part_send_sem, recv_sem=part_recv_sem,
+            device_id=device_of((1 - half) * m + inner), device_id_type=MESH,
         )
 
     def ids_copy(k):
@@ -107,29 +137,62 @@
 
     channel = lax.broadcasted_iota(jnp.int32, (nblk, foot), 1)
 
-    def gather(d):
-        for c in range(chans):
-            r = d * chans + c
+    def gather(dst, d, first, count, base):
+        for c in range(count):
+            r = first + c
             for j in range(nblk):
                 i = rows_sm[j, r]
-                stage_ref[c, pl.ds(j, 1), :] = tile_ref[pl.ds(i, 1), :]
+                stage_ref[base + c, pl.ds(j, 1), :] = tile_ref[pl.ds(i, 1), :]
             column = jnp.sum(
                 jnp.where(channel == r, coef32_ref[...], 0.0), axis=1, keepdims=True
             )
-            send_ref[d, :, c * probe_n : (c + 1) * probe_n] = (stage_ref[c] * column).astype(BF16)
-
-    def launch(k, carry):
-        gather(peer(k)[0])
+            dst[d, :, c * probe_n : (c + 1) * probe_n] = (stage_ref[base + c] * column).astype(BF16)
+
+    def inside(k):
+        return lax.rem(inner + k, m)
+
+    def ids_launch(k, carry):
+        ids_copy(k).start()
+        return carry
+
+    lax.fori_loop(1, n, ids_launch, 0)
+
+    def launch_first(k, carry):
+        q = inside(k)
+        t = (1 - half) * m + q
+        if merge:
+            gather(send_m, q, q * chans_m, chans_m, 0)
+        gather(send_ref, t, m * chans_m + t * chans, chans, chans_m)
 
         @pl.when(k > 1)
         def _():
-            block_copy(k - 1).start()
-            ids_copy(k - 1).start()
-
-        return carry
-
-    lax.fori_loop(1, n + 1, launch, 0)
+            if merge:
+                merge_copy(inside(k - 1)).start()
+            block_copy((1 - half) * m + inside(k - 1)).start()
+
+        return carry
+
+    lax.fori_loop(1, m + 1, launch_first, 0)
+
+    def launch_second(k, carry):
+        t = half * m + inside(k)
+        gather(send_ref, t, m * chans_m + t * chans, chans, 0)
+
+        @pl.when(k == 1)
+        def _():
+            block_copy((1 - half) * m + inner).start()
+
+        @pl.when(k > 1)
+        def _():
+            block_copy(half * m + inside(k - 1)).start()
+
+        return carry
+
+    lax.fori_loop(1, m + 1, launch_second, 0)
     own = pltpu.make_async_copy(send_ref.at[me], recv_ref.at[me], recv_sem.at[me])
+    if merge:
+        own_m = pltpu.make_async_copy(send_m.at[inner], recv_m.at[inner], recv_m_sem.at[inner])
+        own_m.start()
 
     def plane(j, carry):
         at = rows_ref[pl.ds(j, 1), :]
@@ -153,7 +216,7 @@
     own.start()
 
     spd = n_sens // n
-    mine = jnp.where(owner_ref[...] == me, 1.0, 0.0)
+    mine = jnp.where(owner_ref[...] == flat, 1.0, 0.0)
     before = jnp.where(
         lax.broadcasted_iota(jnp.int32, (n_sens, n_sens), 0)
         < lax.broadcasted_iota(jnp.int32, (n_sens, n_sens), 1),
@@ -174,26 +237,44 @@
 
     group = max(1, 256 // nblk)
     depth = group * nblk
-    obs_ref[...] = jnp.zeros_like(obs_ref)
     sensor_up = (lax.broadcasted_iota(jnp.int32, (n_sens, depth), 0) + 1).astype(F32)
 
-    def mix(g, carry):
+    def mix(src, sem, like, obs, start, g):
         pieces = []
         for piece in range(depth // wide):
-            row = ids_recv[g * group + piece * share]
+            row = ids_recv[start + g * group + piece * share]
             for extra in range(1, share):
-                row = row + ids_recv[g * group + piece * share + extra]
+                row = row + ids_recv[start + g * group + piece * share + extra]
             pieces.append(row)
         ids_row = jnp.concatenate(pieces, axis=1)
         mixer = jnp.where(ids_row == sensor_up, 1.0, 0.0).astype(BF16)
         for piece in range(group):
             t = g * group + piece
-            pltpu.make_async_copy(send_ref.at[0], recv_ref.at[t], recv_sem.at[t]).wait()
-        block = recv_ref[pl.ds(g * group, group)].reshape(depth, width)
-        obs_ref[...] += jnp.dot(mixer, block, preferred_element_type=F32)
-        return carry
-
-    lax.fori_loop(0, n // group, mix, 0)
+            pltpu.make_async_copy(like, src.at[t], sem.at[t]).wait()
+        block = src[pl.ds(g * group, group)].reshape(depth, src.shape[2])
+        obs[...] += jnp.dot(mixer, block, preferred_element_type=F32)
+
+    obs_ref[...] = jnp.zeros_like(obs_ref)
+    if merge:
+        obs_m[...] = jnp.zeros_like(obs_m)
+
+        def mix_m(g, carry):
+            mix(recv_m, recv_m_sem, send_m.at[0], obs_m, half * m, g)
+            return carry
+
+        lax.fori_loop(0, m // group, mix_m, 0)
+        away = pl.multiple_of((1 - half) * side, LANES)
+        part_send[...] = obs_m[:, pl.ds(away, side)].astype(BF16)
+        part_copy().start()
+
+    def mix_d(g, carry):
+        mix(recv_ref, recv_sem, send_ref.at[0], obs_ref, 0, g)
+        return carry
+
+    lax.fori_loop(0, n // group, mix_d, 0)
+    if merge:
+        part_copy().wait()
+        keep = pl.multiple_of(half * side, LANES)
 
     eye = lax.broadcasted_iota(jnp.int32, (LANES, LANES), 0) == lax.broadcasted_iota(
         jnp.int32, (LANES, LANES), 1
@@ -201,6 +282,10 @@
     for b in range(n_sens // LANES):
         x = obs_ref[b * LANES : (b + 1) * LANES, :]
         s = jnp.sum(x * x, axis=1, keepdims=True)
+        if merge:
+            rows = pl.ds(b * LANES, LANES)
+            y = obs_m[rows, pl.ds(keep, side)] + part_recv[rows, :].astype(F32)
+            s = s + jnp.sum(y * y, axis=1, keepdims=True)
         h_send[:, b * LANES : (b + 1) * LANES] = jnp.sum(
             jnp.where(eye, s, 0.0), axis=0, keepdims=True
         )
@@ -213,11 +298,18 @@
     lax.fori_loop(1, n, h_launch, 0)
 
     def drain(k, carry):
-        block_copy(k).wait_send()
+        block_copy(peer(k)[0]).wait_send()
         ids_copy(k).wait_send()
         return carry
 
     lax.fori_loop(1, n, drain, 0)
+    if merge:
+
+        def drain_m(k, carry):
+            merge_copy(inside(k)).wait_send()
+            return carry
+
+        lax.fori_loop(1, m, drain_m, 0)
 
     def h_wait(k, carry):
         t = peer(k)[0]
@@ -252,13 +344,26 @@
     tile_r, tile_c, probe_n = probes.shape
     nblk, foot = blk_rows.shape
     n_sens = owner.shape[0]
-    chans = foot // n
+    merge = foot % (2 * n) == 0
+    chans = foot // (2 * n) if merge else foot // n
+    chans_m = 2 * chans if merge else 0
     width = chans * probe_n
     wide = max(LANES, nblk)
 
     vmem = pl.BlockSpec(memory_space=pltpu.VMEM)
     smem = pl.BlockSpec(memory_space=pltpu.SMEM)
     dma = pltpu.SemaphoreType.DMA
+    merge_scratch = []
+    if merge:
+        m = n // 2
+        merge_scratch = [
+            pltpu.VMEM((m, nblk, chans_m * probe_n), BF16),
+            pltpu.VMEM((m, nblk, chans_m * probe_n), BF16),
+            pltpu.VMEM((n_sens, chans_m * probe_n), F32),
+            pltpu.VMEM((n_sens, width), BF16),
+            pltpu.VMEM((n_sens, width), BF16),
+            dma((m,)), dma((m,)), dma, dma,
+        ]
     owned, new, density = pl.pallas_call(
         functools.partial(step_kernel, n, n_gy, 1.0 / (foot * probe_n)),
         out_shape=(
@@ -266,12 +371,12 @@
             jax.ShapeDtypeStruct((1, n_sens), F32),
             jax.ShapeDtypeStruct((tile_r, tile_c), F32),
         ),
-        in_specs=[smem, smem, pl.BlockSpec(memory_space=pl.ANY)] + [vmem] * 5,
+        in_specs=[smem, smem, pl.BlockSpec(memory_space=pltpu.HBM)] + [vmem] * 5,
         out_specs=(vmem, vmem, vmem),
         scratch_shapes=[
             pltpu.VMEM((tile_r, tile_c, probe_n), BF16),
             pltpu.VMEM((tile_r * tile_c, probe_n), F32),
-            pltpu.VMEM((chans, nblk, probe_n), F32),
+            pltpu.VMEM((chans + chans_m, nblk, probe_n), F32),
             pltpu.VMEM((nblk, foot), F32),
             pltpu.VMEM((n, nblk, width), BF16),
             pltpu.VMEM((n, nblk, width), BF16),
@@ -282,9 +387,9 @@
             pltpu.VMEM((1, n_sens), F32),
             pltpu.VMEM((n, 1, n_sens), F32),
             dma((4,)), dma((n,)), dma((n,)), dma((n,)), dma((n,)), dma((n,)), dma((n,)),
-        ],
+        ] + merge_scratch,
         compiler_params=pltpu.CompilerParams(
-            collective_id=0, has_side_effects=True, vmem_limit_bytes=61 * 2**20
+            collective_id=0, has_side_effects=True, vmem_limit_bytes=56 * 2**20
         ),
         name="reweight_step",
     )(

time: 70.7 us -> 59.5 us (0.84)
  Pallas kernels: 65.3 us -> 54.1 us
    pallas_call x1, Pallas kernels: 65.3 us -> 54.1 us  [local(): pl.pallas_call(functools.partial(step_kernel, n, n_gy, 1.0 / (foot * prob...]
where the time goes in v3:
time: 59.5 us; the launch traced here: 59.2 us
  Pallas kernels  54.1 us (91%)
  local copies, waits for them, and re-layouts  3.75 us (6%)
  between operations  1.29 us (2%)
    pallas_call x1, Pallas kernels, local(): pl.pallas_call(functools.partial(step_kernel, n, n_gy, 1.0 / (foot * prob...  54.1 us
    unnamed x3, local copies, waits for them, and re-layouts  3.75 us

profile of v3, /device:TPU:0, one launch (start us, length us, event | category | flops | bytes accessed | tf_op | source)
XLA Modules:
  0.0 59.2 jit_solution(16070400400167457937)
XLA Ops:
  1.3 54.1 %reweight_step.1 = (f32[1,8]{1,0:T(1,128)}, f32[1,256]{1,0:T(1,128)}, f32[32,256]{1,0:T(8,128)}) custom-call(s32[32,128]{1,0:T(8,128)} %rows_ref.1, s32[1]{0:T(128)S(6)} %copy.13.count_sm, bf16[32,256,256]{2,1,0:T(8,128)(2,1)} %probes_hbm.1, s32[1,32]{1,0:T(1,128)} %bitcast.8, s32[32,128]{1,0:T(8,128)} %rows_ref.1, bf16[32,128]{1,0:T(8,128)(2,1)} %coef_ref.1, ...), custom_call_target="tpu_custom_call" | custom-call | tf_op jit(solution)/shard_map/reweight_step/pallas_call | solution.py:367
  55.4 1.1 %copy.14 = f32[8]{0:T(128)} copy(f32[8]{0:T(128)} %bitcast.9) | data formatting | bytes 64
  56.6 1.2 %copy.15 = f32[256]{0:T(256)} copy(f32[256]{0:T(256)} %bitcast.7) | data formatting | bytes 2048
  57.8 1.4 %copy.16 = f32[32,256]{1,0:T(8,128)} copy(f32[32,256]{1,0:T(8,128)} %get-tuple-element.14) | data formatting | bytes 65536
